TPU v7x, 256 devices: a whole 4x4x8 slice. The times are simulated.
256 devices in a mesh: pair: 32 (over x, z_hi, core), aux: 8 (over z_lo, y).
Axes of the slice: x: 4, y: 4, z: 8 (z_hi: 4, z_lo: 2; z = z_hi * 2 + z_lo), core: 2. Of those that a mesh axis runs over, the one named last changes fastest.
Arguments:
- integrals: float32 [32, 640, 4096], P(None, 'aux', 'pair'), may hold values from -6 to 6
- factor: float32 [4096, 4096], P('aux', 'pair'), may hold values from -1 to 2, as said below
- diag_inverse: float32 [8, 512, 512], P('aux'), may hold values from -1 to 1, as said below
Outputs:
- transformed: float32 [32, 640, 4096], P('pair', None, 'aux')
Inputs may be any that keep to these rules, and one draw needn't show every extreme that they name: factor is zero above its diagonal. diag_inverse[j] is the inverse, up to rounding, of the factor's j-th diagonal block of 512 x 512.
All inputs are finite; a program needn't handle non-finite values.
Results may differ from a plain program's by a relative error of at most 0.0001.
Values sent between devices are 32-bit elements; how exact they have to be, the bound alone decides.
No kernel may reach another device: no remote copies, remote signals or barrier semaphores. Data moves between devices by JAX's collectives and lax.ppermute only.
A program may use at most 128 MiB of HBM per device.

v0:
```python
import jax
import jax.numpy as jnp
from jax import lax
from jax.sharding import PartitionSpec as P


def from_root(x, axis, root):
    mine = lax.axis_index(axis) == root
    return lax.psum(jnp.where(mine, x, jnp.zeros_like(x)), axis)


def product(left, right):
    return jnp.dot(left, right, precision=lax.Precision.HIGHEST, preferred_element_type=jnp.float32)


def local(integrals, factor, diag_inverse):
    relaid = lax.all_to_all(
        lax.all_to_all(integrals, "pair", split_axis=0, concat_axis=2, tiled=True),
        "aux",
        split_axis=2,
        concat_axis=1,
        tiled=True,
    )
    occ_count, virt_count, panel_width = relaid.shape
    remain = relaid.reshape(occ_count * virt_count, panel_width)
    row_panel = lax.all_gather(factor, "pair", axis=1, tiled=True)
    inverse_t = diag_inverse[0].T
    own_index = lax.axis_index("aux")
    panel_count = lax.axis_size("aux")
    result = jnp.zeros_like(remain)
    for step in range(panel_count):
        result = lax.cond(own_index == step, lambda: product(remain, inverse_t), lambda: result)
        if step + 1 < panel_count:
            factor_block = row_panel[:, step * panel_width : (step + 1) * panel_width].T
            arrived = from_root(result, "aux", step)
            remain = lax.cond(
                own_index > step, lambda: remain - product(arrived, factor_block), lambda: remain
            )
    return result.reshape(occ_count, virt_count, panel_width)


def solution(mesh):
    in_specs = (P(None, "aux", "pair"), P("aux", "pair"), P("aux", None, None))
    out_specs = P("pair", None, "aux")
    return jax.shard_map(local, mesh=mesh, in_specs=in_specs, out_specs=out_specs, check_vma=False)
```

profile of v0, /device:TPU:56, one launch (start us, length us, event | category | flops | bytes accessed | tf_op | source)
XLA Modules:
  0.0 783.9 jit_solution(10869943194843136534)
XLA Ops:
  7.4 1.8 copy.26
  9.2 53.9 %all_to_all.33 = f32[32,80,128]{2,1,0:T(8,128)S(1)} all-to-all(f32[32,80,128]{2,1,0:T(8,128)} %param.33), channel_id=1, replica_groups=mesh['pair'=32,'aux'=8] {'pair'}, dimensions={0} | all-to-all | bytes 2621440 | tf_op jit(solution)/shard_map/all_to_all | solution.py:18
  63.5 5.1 copy.22
  68.7 5.7 all-to-all-start.1
  74.7 52.9 %all-to-all-done.1 = f32[1,80,4096]{1,0,2:T(1,128)} async-done(((f32[1,80,4096]{1,0,2:T(1,128)}), f32[1,80,4096]{1,0,2:T(1,128)}, u32[]{:S(2)}, u32[]{:S(2)}) %all-to-all-start.1) | async-done | bytes 1310752 | tf_op jit(solution)/shard_map/all_to_all | solution.py:17
  127.6 2.8 copy.27
  130.4 2.1 copy.24
  132.5 1.2 conditional.15
  135.0 6.2 slice_bitcast_fusion
  141.2 77.3 %all-reduce.8.cloned.1.call-done = f32[640,512]{1,0:T(8,128)} async-done(((f32[640,512]{1,0:T(8,128)}), f32[640,512]{1,0:T(8,128)}) %all-reduce.8.cloned.1.call-update) | async-done | bytes 1310736 | tf_op jit(solution)/shard_map/psum | solution.py:9
  218.5 4.0 conditional.16
  218.5 4.0 convolution_subtract_fusion
  223.8 85.2 %all-reduce.10.cloned.1.call-done = f32[640,512]{1,0:T(8,128)} async-done(((f32[640,512]{1,0:T(8,128)}), f32[640,512]{1,0:T(8,128)}) %all-reduce.10.cloned.1.call-update) | async-done | bytes 1310736 | tf_op jit(solution)/shard_map/psum | solution.py:9
  309.0 4.2 conditional.18
  309.2 4.0 convolution_subtract_fusion.1
  314.5 87.7 %all-reduce.12.cloned.1.call-done = f32[640,512]{1,0:T(8,128)} async-done(((f32[640,512]{1,0:T(8,128)}), f32[640,512]{1,0:T(8,128)}) %all-reduce.12.cloned.1.call-update) | async-done | bytes 1310736 | tf_op jit(solution)/shard_map/psum | solution.py:9
  402.2 4.0 conditional.20
  402.2 4.0 convolution_subtract_fusion.2
  407.5 87.1 %all-reduce.14.cloned.1.call-done = f32[640,512]{1,0:T(8,128)} async-done(((f32[640,512]{1,0:T(8,128)}), f32[640,512]{1,0:T(8,128)}) %all-reduce.14.cloned.1.call-update) | async-done | bytes 1310736 | tf_op jit(solution)/shard_map/psum | solution.py:9
  494.6 4.0 conditional.22
  494.6 4.0 convolution_subtract_fusion.3
  500.1 86.0 %all-reduce.16.cloned.1.call-done = f32[640,512]{1,0:T(8,128)} async-done(((f32[640,512]{1,0:T(8,128)}), f32[640,512]{1,0:T(8,128)}) %all-reduce.16.cloned.1.call-update) | async-done | bytes 1310736 | tf_op jit(solution)/shard_map/psum | solution.py:9
  586.2 4.0 conditional.24
  586.2 4.0 convolution_subtract_fusion.4
  591.5 85.0 %all-reduce.18.cloned.1.call-done = f32[640,512]{1,0:T(8,128)} async-done(((f32[640,512]{1,0:T(8,128)}), f32[640,512]{1,0:T(8,128)}) %all-reduce.18.cloned.1.call-update) | async-done | bytes 1310736 | tf_op jit(solution)/shard_map/psum | solution.py:9
  676.5 4.0 conditional.26
  676.5 4.0 convolution_subtract_fusion.5
  681.8 87.0 %all-reduce.20.cloned.1.call-done = f32[640,512]{1,0:T(8,128)} async-done(((f32[640,512]{1,0:T(8,128)}), f32[640,512]{1,0:T(8,128)}) %all-reduce.20.cloned.1.call-update) | async-done | bytes 1310736 | tf_op jit(solution)/shard_map/psum | solution.py:9
  768.7 4.0 conditional.28
  769.0 3.7 convolution_subtract_fusion.6
  772.7 3.3 conditional.29
  772.7 3.3 convolution_bitcast_fusion
  (35 shorter events, 11.1 us)
Async XLA Ops:
  7.4 127.7 %all-gather.2.cloned.1.call-start = ((), (), s32[]{:S(2)}) async-start(), calls=%async_computation.3 | async-start | bytes 8650752 | tf_op jit(solution)/shard_map/all_gather | solution.py:26
  68.7 5.7 copy-start
  68.7 59.0 %all-to-all-start.1 = ((f32[1,80,4096]{1,0,2:T(1,128)}), f32[1,80,4096]{1,0,2:T(1,128)}, u32[]{:S(2)}, u32[]{:S(2)}) async-start(f32[1,80,4096]{1,0,2:T(1,128)} %copy.22), calls=%async_computation.1 | async-start | bytes 4194304 | tf_op jit(solution)/shard_map/all_to_all | solution.py:17
  74.4 144.1 %all-reduce.8.cloned.1.call-start = ((), (), s32[]{:S(2)}) async-start(), calls=%async_computation.2 | async-start | bytes 2621440 | tf_op jit(solution)/shard_map/psum | solution.py:9
  135.0 174.1 %all-reduce.10.cloned.1.call-start = ((), (), s32[]{:S(2)}) async-start(), calls=%async_computation.4 | async-start | bytes 2621440 | tf_op jit(solution)/shard_map/psum | solution.py:9
  223.7 178.4 %all-reduce.12.cloned.1.call-start = ((), (), s32[]{:S(2)}) async-start(), calls=%async_computation.5 | async-start | bytes 2621440 | tf_op jit(solution)/shard_map/psum | solution.py:9
  314.5 180.1 %all-reduce.14.cloned.1.call-start = ((), (), s32[]{:S(2)}) async-start(), calls=%async_computation.6 | async-start | bytes 2621440 | tf_op jit(solution)/shard_map/psum | solution.py:9
  407.5 178.7 %all-reduce.16.cloned.1.call-start = ((), (), s32[]{:S(2)}) async-start(), calls=%async_computation.7 | async-start | bytes 2621440 | tf_op jit(solution)/shard_map/psum | solution.py:9
  500.1 176.4 %all-reduce.18.cloned.1.call-start = ((), (), s32[]{:S(2)}) async-start(), calls=%async_computation.8 | async-start | bytes 2621440 | tf_op jit(solution)/shard_map/psum | solution.py:9
  591.4 177.3 %all-reduce.20.cloned.1.call-start = ((), (), s32[]{:S(2)}) async-start(), calls=%async_computation.9 | async-start | bytes 2621440 | tf_op jit(solution)/shard_map/psum | solution.py:9
Sparse Core Ops, SparseCore 0:
  10.7 112.6 all-gather.1
Sparse Core Ops, SparseCore 1:
  135.0 83.4 all-reduce.7
  223.8 85.1 all-reduce.9
  314.5 87.6 all-reduce.11
  407.6 87.0 all-reduce.13
  500.2 86.0 all-reduce.15
  591.5 84.9 all-reduce.17
  681.9 86.8 all-reduce.19
where the time goes:
time: 792 us; the launch traced here: 784 us
  waiting for transfers between devices  648 us (82%)
  blocking collectives  53.9 us (7%)
  matrix products  31.2 us (4%)
  local copies, waits for them, and re-layouts  19.9 us (3%)
  between operations  15.6 us (2%)
  other arithmetic  8.41 us (1%)
    psum x7, waiting for transfers between devices, from_root(): return lax.psum(jnp.where(mine, x, jnp.zeros_like(x)), axis)  595 us
    all_to_all x1, blocking collectives, local(): lax.all_to_all(integrals, 'pair', split_axis=0, concat_axis=2, tiled=True)  53.9 us
    all_to_all x1, waiting for transfers between devices, local(): lax.all_to_all(lax.all_to_all(integrals, 'pair', split_axis=0, concat_axi...  52.9 us
    dot_general x8, matrix products, product(): jnp.dot(left, right, precision=lax.Precision.HIGHEST, preferred_element_t...  31.2 us
  transfers between devices with their start and end apart: 9, of which 8 were waited for; matrix products, arithmetic and copies ran while one was open for 2% of the time, Pallas kernels for 0%

commit v1 on v0

v1 whole, which is shorter than its diff:
```python
import functools
import jax
import jax.numpy as jnp
from jax import lax
from jax.experimental import pallas as pl
from jax.experimental.pallas import tpu as pltpu
from jax.sharding import PartitionSpec as P

NX, NY, NZ = 4, 4, 8
ALL = ("pair", "aux")
EARLY, LATE = 5, 4
SLOTS = EARLY + LATE
PANELS, PANEL, LANES, ROWS = 8, 512, 128, 80
STEPS = (0, -1, 1, 2)


def device_id(x, y, z, core):
    return ((x * NZ // 2 + z // 2) * 2 + core) * 8 + (z % 2) * NY + y


def shift(value, dx=0, dy=0, dz=0, core=0):
    pairs = [
        (device_id(x, y, z, c), device_id((x + dx) % NX, (y + dy) % NY, (z + dz) % NZ, (c + core) % 2))
        for x in range(NX)
        for y in range(NY)
        for z in range(NZ)
        for c in range(2)
    ]
    return lax.ppermute(value, ALL, pairs)


def along(axis):
    return lambda value, d: shift(value, **{axis: d})


def rings(block, first, second):
    one, two = along(first), along(second)
    up, down = one(block, 1), one(block, -1)
    far = jnp.concatenate([one(up[:4], 1), one(down[4:], -1)])
    whole = jnp.stack([block, up, down, far])
    up, down = two(whole, 1), two(whole, -1)
    far_up, far_down = two(up[:2], 1), two(down[2:], -1)
    return [whole, up, down, far_up, far_down]


def pieces(factor, diag_inverse, pair, aux):
    column = pair // 4
    diagonal = lax.dynamic_slice(diag_inverse[0], (0, LANES * (pair % 4)), (PANEL, LANES))
    slab = jnp.where(column == aux, diagonal, factor)
    chunks = slab.reshape(2, 8, 32, LANES).transpose(1, 0, 2, 3)
    chunks = lax.all_to_all(chunks, "aux", 0, 0, tiled=True)
    own = chunks[:, 0]
    other = lax.ppermute(chunks[:, 1], "pair", [(p, 31 - p) for p in range(32)])
    is_low = column < 4
    low = jnp.where(is_low, own, other)
    high = jnp.where(is_low, other, own)
    both = jnp.concatenate([low, high])
    least = jnp.minimum(column, 7 - column)
    held = []
    for slot in range(SLOTS):
        paired = (slot + 7) // 2 if slot % 2 else 8 + (slot + 6) // 2
        index = jnp.where(slot < 7 - 2 * least, slot + least, paired)
        held.append(lax.dynamic_index_in_dim(both, index, 0, keepdims=False))
    return jnp.stack(held)


def kernel(*refs):
    place_ref, x_ref = refs[:2]
    arrays = refs[2:22]
    out_ref, held, remain, parts, early_sem, late_sem = refs[22:]
    x, y, z, core = (place_ref[i] for i in range(4))

    def fetch(sources, dx, dy, from_core, first_slot, sem):
        sx, sy = lax.rem(x + dx + NX, NX), lax.rem(y + dy + NY, NY)

        @pl.loop(0, NZ)
        def _(dz):
            sz = lax.rem(z - dz + NZ, NZ)
            holder = sx * 8 + lax.div(sz, 2) * 2 + from_core
            group = lax.rem(sz, 2) * NY + sy
            count = sources.shape[1]
            pltpu.make_async_copy(
                sources.at[dz], held.at[holder, pl.ds(first_slot, count), group], sem
            ).start()

    def fetch_all(five, from_core, first_slot, sem, order):
        for number, (ref, second, blocks) in enumerate(
            zip(five, (0, -1, 1, -2, 2), ((0, 1, 2, 3),) * 3 + ((0, 1), (2, 3)), strict=True)
        ):
            for at, block in enumerate(blocks):
                first = STEPS[block]
                dx, dy = (first, second) if order == "xy" else (second, first)
                fetch(ref.at[at], dx, dy, from_core, first_slot, sem)

    fetch_all(arrays[0:5], core, 0, early_sem, "xy")
    fetch_all(arrays[5:10], 1 - core, 0, early_sem, "xy")
    fetch_all(arrays[10:15], core, EARLY, late_sem, "yx")
    fetch_all(arrays[15:20], 1 - core, EARLY, late_sem, "yx")

    def product(left, j, k):
        low_slot = jnp.where(j < 7 - k, j - k, 2 * j - 7)
        slot = jnp.where(k < 4, low_slot, 2 * j - 6)
        halves = []
        for half in range(2):
            total = None
            for pair in range(2):
                tiles = []
                for s in range(2):
                    p = 4 * k + 2 * pair + s
                    holder = 31 - p if half else p
                    tiles.append(held[holder, slot].reshape(256, LANES))
                weight = jnp.concatenate(tiles, axis=1)
                high = weight.astype(jnp.bfloat16)
                low = (weight - high.astype(jnp.float32)).astype(jnp.bfloat16)
                part = left[:, 256 * pair : 256 * (pair + 1)]
                dims = (((1,), (1,)), ((), ()))
                twice = lax.dot_general(part, high, dims, preferred_element_type=jnp.float32)
                once = lax.dot_general(part[:ROWS], low, dims, preferred_element_type=jnp.float32)
                piece = twice[:ROWS] + (twice[ROWS:] + once)
                total = piece if total is None else total + piece
            halves.append(total)
        return jnp.concatenate(halves, axis=1)

    def split(value):
        high = value.astype(jnp.bfloat16)
        low = (value - high.astype(jnp.float32)).astype(jnp.bfloat16)
        return jnp.concatenate([high, low], axis=0)

    def panel(j, carry):
        remain[...] = jnp.concatenate([x_ref[4 * j + s] for s in range(4)], axis=1)

        def update(k, carry):
            remain[...] -= product(parts[k], j, k)
            return carry

        lax.fori_loop(0, j, update, 0)
        solved = product(split(remain[...]), j, j)
        out_ref[j] = solved
        parts[j] = split(solved)
        return carry

    early = held.at[:, pl.ds(0, EARLY)]
    pltpu.make_async_copy(early, early, early_sem).wait()
    lax.fori_loop(0, EARLY, panel, 0)
    late = held.at[:, pl.ds(EARLY, LATE)]
    pltpu.make_async_copy(late, late, late_sem).wait()
    lax.fori_loop(EARLY, PANELS, panel, 0)


def solve(place, rows, arrays):
    return pl.pallas_call(
        kernel,
        out_shape=jax.ShapeDtypeStruct((PANELS, ROWS, PANEL), jnp.float32),
        in_specs=[pl.BlockSpec(memory_space=pltpu.SMEM), pl.BlockSpec(memory_space=pltpu.VMEM)]
        + [pl.BlockSpec(memory_space=pltpu.HBM)] * len(arrays),
        out_specs=pl.BlockSpec(memory_space=pltpu.VMEM),
        scratch_shapes=[
            pltpu.VMEM((32, SLOTS, 8, 32, LANES), jnp.float32),
            pltpu.VMEM((ROWS, PANEL), jnp.float32),
            pltpu.VMEM((PANELS, 2 * ROWS, PANEL), jnp.bfloat16),
            pltpu.SemaphoreType.DMA,
            pltpu.SemaphoreType.DMA,
        ],
        compiler_params=pltpu.CompilerParams(vmem_limit_bytes=48 * 2**20),
        cost_estimate=pl.CostEstimate(flops=16 * 10**9, bytes_accessed=40 * 10**6, transcendentals=0),
    )(place, rows, *arrays)


def local(integrals, factor, diag_inverse):
    pair, aux = lax.axis_index("pair"), lax.axis_index("aux")
    x, z, core = pair // 8, (pair // 2) % 4 * 2 + aux // NY, pair % 2
    place = jnp.stack([x, aux % NY, z, core]).astype(jnp.int32)

    piece = pieces(factor, diag_inverse, pair, aux)
    column = jnp.stack([piece] + [shift(piece, dz=d) for d in range(1, NZ)])
    early = rings(column[:, :EARLY], "dx", "dy")
    late = rings(column[:, EARLY:], "dy", "dx")
    rows = lax.all_to_all(integrals, "pair", 0, 0, tiled=True)
    arrays = early + [shift(v, core=1) for v in early] + late + [shift(v, core=1) for v in late]
    solved = solve(place, rows, arrays)
    result = lax.all_to_all(solved, "aux", 0, 0, tiled=True)
    return result.reshape(1, 8 * ROWS, PANEL)


def solution(mesh):
    in_specs = (P(None, "aux", "pair"), P("aux", "pair"), P("aux", None, None))
    out_specs = P("pair", None, "aux")
    return jax.shard_map(local, mesh=mesh, in_specs=in_specs, out_specs=out_specs, check_vma=False)
```

time: 792 us -> 340 us (0.43)
  waiting for transfers between devices: 648 us -> 215 us
  starting transfers between devices: 6 us -> 52.5 us
  matrix products: 31.2 us -> 0 us
  Pallas kernels: 0 us -> 26.5 us
  blocking collectives: 53.9 us -> 30.6 us
  between operations: 15.6 us -> 0.43 us
  local copies, waits for them, and re-layouts: 19.9 us -> 10.6 us
    psum x7 -> x0, waiting for transfers between devices: 595 us -> none  [from_root(): return lax.psum(jnp.where(mine, x, jnp.zeros_like(x)), axis)]
    ppermute x0 -> x34, waiting for transfers between devices: none -> 186 us  [the longest x33 179 us: shift(): return lax.ppermute(value, ALL, pairs)]
    ppermute x0 -> x34, starting transfers between devices: none -> 47.8 us  [the longest x33 42.1 us: shift(): return lax.ppermute(value, ALL, pairs)]
    dot_general x8 -> x0, matrix products: 31.2 us -> none  [product(): jnp.dot(left, right, precision=lax.Precision.HIGHEST, preferred_element_t...]
    pallas_call x0 -> x1, Pallas kernels: none -> 26.5 us  [solve(): pl.pallas_call(kernel, out_shape=jax.ShapeDtypeStruct((PANELS, ROWS, PANE...]
    all_to_all x1, waiting for transfers between devices: 52.9 us -> 28.8 us  [local(): rows = lax.all_to_all(integrals, 'pair', 0, 0, tiled=True)]
    all_to_all x1 -> x2, blocking collectives: 53.9 us -> 30.6 us  [the longest x1 20.6 us: local(): result = lax.all_to_all(solved, 'aux', 0, 0, tiled=True)]
    all_to_all x4 -> x0, local copies, waits for them, and re-layouts: 10.4 us -> none  [the longest x2 5.55 us: local(): lax.all_to_all(integrals, 'pair', split_axis=0, concat_axis=2, tiled=True)]
  transfers between devices with their start and end apart: 9 -> 35, of which waited for: 8 -> 17; matrix products, arithmetic and copies ran while one was open for 2% -> 2% of each run, Pallas kernels for 0% -> 0%
where the time goes in v1:
time: 340 us; the launch traced here: 337 us
  waiting for transfers between devices  215 us (63%)
  starting transfers between devices  52.5 us (15%)
  blocking collectives  30.6 us (9%)
  Pallas kernels  26.5 us (8%)
  local copies, waits for them, and re-layouts  10.6 us (3%)
    ppermute x33, waiting for transfers between devices, shift(): return lax.ppermute(value, ALL, pairs)  179 us
    ppermute x33, starting transfers between devices, shift(): return lax.ppermute(value, ALL, pairs)  42.1 us
    all_to_all x1, waiting for transfers between devices, local(): rows = lax.all_to_all(integrals, 'pair', 0, 0, tiled=True)  28.8 us
    pallas_call x1, Pallas kernels, solve(): pl.pallas_call(kernel, out_shape=jax.ShapeDtypeStruct((PANELS, ROWS, PANE...  26.5 us
    all_to_all x1, blocking collectives, local(): result = lax.all_to_all(solved, 'aux', 0, 0, tiled=True)  20.6 us
    all_to_all x1, blocking collectives, pieces(): chunks = lax.all_to_all(chunks, 'aux', 0, 0, tiled=True)  10 us
  transfers between devices with their start and end apart: 35, of which 17 were waited for; matrix products, arithmetic and copies ran while one was open for 2% of the time, Pallas kernels for 0%

profile of v1, /device:TPU:56, one launch (start us, length us, event | category | flops | bytes accessed | tf_op | source)
XLA Modules:
  0.0 337.1 jit_solution(3628625275724027602)
XLA Ops:
  1.1 10.0 %all_to_all.15 = f32[8,2,32,128]{3,2,1,0:T(8,128)S(1)} all-to-all(f32[8,2,32,128]{3,2,1,0:T(8,128)S(1)} %copy.6), channel_id=1, replica_groups=mesh['pair'=32,'aux'=8] {'aux'}, dimensions={0} | all-to-all | bytes 524288 | tf_op jit(solution)/shard_map/all_to_all | solution.py:51
  11.1 5.7 %collective-permute-start = (f32[8,32,128]{2,1,0:T(8,128)S(1)}, f32[8,32,128]{2,1,0:T(8,128)S(1)}, u32[]{:S(2)}, u32[]{:S(2)}) collective-permute-start(f32[8,32,128]{2,1,0:T(8,128)S(1)} %slice_bitcast_fusion), channel_id=1, source_target_pairs={{0,248},{8,240},{16,232},{24,224},{32,216},{40,208},{48,200},{56,1... | collective-permute-start | bytes 393224 | tf_op jit(solution)/shard_map/ppermute | solution.py:53
  16.8 6.7 %collective-permute-done = f32[8,32,128]{2,1,0:T(8,128)S(1)} collective-permute-done((f32[8,32,128]{2,1,0:T(8,128)S(1)}, f32[8,32,128]{2,1,0:T(8,128)S(1)}, u32[]{:S(2)}, u32[]{:S(2)}) %collective-permute-start) | collective-permute-done | bytes 131104 | tf_op jit(solution)/shard_map/ppermute | solution.py:53
  24.1 5.1 %collective-permute-start.6 = (f32[9,32,128]{2,1,0:T(8,128)S(1)}, f32[9,32,128]{2,1,0:T(8,128)S(1)}, u32[]{:S(2)}, u32[]{:S(2)}) collective-permute-start(f32[9,32,128]{2,1,0:T(8,128)S(1)} %constant_dynamic-update-slice_fusion), channel_id=1, source_target_pairs={{0,48},{8,56},{4,52},{12,60},{16,0},{24,8},{20,4},{28,12},{32,16},... | collective-permute-start | bytes 442376 | tf_op jit(solution)/shard_map/ppermute | solution.py:29
  29.8 2.3 collective-permute-start.4
  33.3 11.2 %collective-permute-done.1 = f32[9,32,128]{2,1,0:T(8,128)S(1)} collective-permute-done((f32[9,32,128]{2,1,0:T(8,128)S(1)}, f32[9,32,128]{2,1,0:T(8,128)S(1)}, u32[]{:S(2)}, u32[]{:S(2)}) %collective-permute-start.1) | collective-permute-done | bytes 147488 | tf_op jit(solution)/shard_map/ppermute | solution.py:29
  44.5 10.2 %collective-permute-done.2 = f32[9,32,128]{2,1,0:T(8,128)S(1)} collective-permute-done((f32[9,32,128]{2,1,0:T(8,128)S(1)}, f32[9,32,128]{2,1,0:T(8,128)S(1)}, u32[]{:S(2)}, u32[]{:S(2)}) %collective-permute-start.2) | collective-permute-done | bytes 147488 | tf_op jit(solution)/shard_map/ppermute | solution.py:29
  54.7 2.0 collective-permute-start.3
  56.7 12.0 %collective-permute-done.3 = f32[9,32,128]{2,1,0:T(8,128)S(1)} collective-permute-done((f32[9,32,128]{2,1,0:T(8,128)S(1)}, f32[9,32,128]{2,1,0:T(8,128)S(1)}, u32[]{:S(2)}, u32[]{:S(2)}) %collective-permute-start.3) | collective-permute-done | bytes 147488 | tf_op jit(solution)/shard_map/ppermute | solution.py:29
  68.9 2.8 collective-permute-start.21
  71.8 11.1 %collective-permute-done.21 = f32[8,4,32,128]{3,2,1,0:T(8,128)S(1)} collective-permute-done((f32[8,4,32,128]{3,2,1,0:T(8,128)S(1)}, f32[8,4,32,128]{3,2,1,0:T(8,128)S(1)}, u32[]{:S(2)}, u32[]{:S(2)}) %collective-permute-start.21) | collective-permute-done | bytes 524320 | tf_op jit(solution)/shard_map/ppermute | solution.py:29
  82.9 3.8 %collective-permute-start.23 = (f32[4,4,32,128]{3,2,1,0:T(8,128)S(1)}, f32[4,4,32,128]{3,2,1,0:T(8,128)S(1)}, u32[]{:S(2)}, u32[]{:S(2)}) collective-permute-start(f32[4,4,32,128]{3,2,1,0:T(8,128)S(1)} %slice.56), channel_id=1, source_target_pairs={{0,1},{8,9},{4,5},{12,13},{16,17},{24,25},{20,21},{28,29},{32,33},... | collective-permute-start | bytes 786440 | tf_op jit(solution)/shard_map/ppermute | solution.py:29
  87.3 3.0 collective-permute-start.9
  91.3 3.5 %collective-permute-done.24 = f32[4,4,32,128]{3,2,1,0:T(8,128)S(1)} collective-permute-done((f32[4,4,32,128]{3,2,1,0:T(8,128)S(1)}, f32[4,4,32,128]{3,2,1,0:T(8,128)S(1)}, u32[]{:S(2)}, u32[]{:S(2)}) %collective-permute-start.24) | collective-permute-done | bytes 262176 | tf_op jit(solution)/shard_map/ppermute | solution.py:29
  95.1 3.4 %collective-permute-start.26 = (f32[4,8,4,32,128]{4,3,2,1,0:T(8,128)S(1)}, f32[4,8,4,32,128]{4,3,2,1,0:T(8,128)}, u32[]{:S(2)}, u32[]{:S(2)}) collective-permute-start(f32[4,8,4,32,128]{4,3,2,1,0:T(8,128)S(1)} %pad_maximum_fusion.1.refs_12_), channel_id=1, source_target_pairs={{0,192},{8,200},{4,196},{12,204},{16,208},{24,216},{20,212},{28,22... | collective-permute-start | bytes 6291464 | tf_op jit(solution)/shard_map/ppermute | solution.py:29
  98.5 5.4 %collective-permute-done.8 = f32[8,5,32,128]{3,2,1,0:T(8,128)S(1)} collective-permute-done((f32[8,5,32,128]{3,2,1,0:T(8,128)S(1)}, f32[8,5,32,128]{3,2,1,0:T(8,128)S(1)}, u32[]{:S(2)}, u32[]{:S(2)}) %collective-permute-start.8) | collective-permute-done | bytes 655392 | tf_op jit(solution)/shard_map/ppermute | solution.py:29
  105.4 3.8 %collective-permute-start.11 = (f32[4,5,32,128]{3,2,1,0:T(8,128)S(1)}, f32[4,5,32,128]{3,2,1,0:T(8,128)S(1)}, u32[]{:S(2)}, u32[]{:S(2)}) collective-permute-start(f32[4,5,32,128]{3,2,1,0:T(8,128)S(1)} %slice.52), channel_id=1, source_target_pairs={{0,192},{8,200},{4,196},{12,204},{16,208},{24,216},{20,212},{28,22... | collective-permute-start | bytes 983048 | tf_op jit(solution)/shard_map/ppermute | solution.py:29
  109.2 4.0 %collective-permute-done.10 = f32[4,5,32,128]{3,2,1,0:T(8,128)S(1)} collective-permute-done((f32[4,5,32,128]{3,2,1,0:T(8,128)S(1)}, f32[4,5,32,128]{3,2,1,0:T(8,128)S(1)}, u32[]{:S(2)}, u32[]{:S(2)}) %collective-permute-start.10) | collective-permute-done | bytes 327712 | tf_op jit(solution)/shard_map/ppermute | solution.py:29
  113.1 42.1 %collective-permute-done.11 = f32[4,5,32,128]{3,2,1,0:T(8,128)S(1)} collective-permute-done((f32[4,5,32,128]{3,2,1,0:T(8,128)S(1)}, f32[4,5,32,128]{3,2,1,0:T(8,128)S(1)}, u32[]{:S(2)}, u32[]{:S(2)}) %collective-permute-start.11) | collective-permute-done | bytes 327712 | tf_op jit(solution)/shard_map/ppermute | solution.py:29
  155.7 3.2 collective-permute-start.12
  158.9 1.8 collective-permute-start.25
  162.2 51.5 %collective-permute-done.13.refs_4_ = f32[4,8,5,32,128]{4,3,2,1,0:T(8,128)} collective-permute-done((f32[4,8,5,32,128]{4,3,2,1,0:T(8,128)S(1)}, f32[4,8,5,32,128]{4,3,2,1,0:T(8,128)}, u32[]{:S(2)}, u32[]{:S(2)}) %collective-permute-start.13) | collective-permute-done | bytes 2621472 | tf_op jit(solution)/shard_map/ppermute | solution.py:29
  213.7 3.7 %collective-permute-start.28 = (f32[2,8,4,32,128]{4,3,2,1,0:T(8,128)S(1)}, f32[2,8,4,32,128]{4,3,2,1,0:T(8,128)S(1)}, u32[]{:S(2)}, u32[]{:S(2)}) collective-permute-start(f32[2,8,4,32,128]{4,3,2,1,0:T(8,128)S(1)} %slice.59), channel_id=1, source_target_pairs={{0,192},{8,200},{4,196},{12,204},{16,208},{24,216},{20,212},{28,22... | collective-permute-start | bytes 3145736 | tf_op jit(solution)/shard_map/ppermute | solution.py:29
  219.0 3.0 slice.53
  222.1 2.7 collective-permute-start.14
  224.9 12.2 %collective-permute-done.28.refs_16_ = f32[2,8,4,32,128]{4,3,2,1,0:T(8,128)S(1)} collective-permute-done((f32[2,8,4,32,128]{4,3,2,1,0:T(8,128)S(1)}, f32[2,8,4,32,128]{4,3,2,1,0:T(8,128)S(1)}, u32[]{:S(2)}, u32[]{:S(2)}) %collective-permute-start.28) | collective-permute-done | bytes 1048608 | tf_op jit(solution)/shard_map/ppermute | solution.py:29
  237.1 10.2 %collective-permute-done.27.refs_15_ = f32[2,8,4,32,128]{4,3,2,1,0:T(8,128)S(1)} collective-permute-done((f32[2,8,4,32,128]{4,3,2,1,0:T(8,128)S(1)}, f32[2,8,4,32,128]{4,3,2,1,0:T(8,128)S(1)}, u32[]{:S(2)}, u32[]{:S(2)}) %collective-permute-start.27) | collective-permute-done | bytes 1048608 | tf_op jit(solution)/shard_map/ppermute | solution.py:29
  248.9 4.7 %all-to-all-start = ((f32[32,80,128]{2,1,0:T(8,128)}), f32[32,80,128]{2,1,0:T(8,128)}, u32[]{:S(2)}, u32[]{:S(2)}) async-start(f32[32,80,128]{2,1,0:T(8,128)} %param.3), calls=%async_computation | async-start | bytes 2621440 | tf_op jit(solution)/shard_map/all_to_all | solution.py:178
  254.5 3.2 collective-permute-done.32.refs_20_
  258.9 28.8 %all-to-all-done.refs_1_ = f32[32,80,128]{2,1,0:T(8,128)} async-done(((f32[32,80,128]{2,1,0:T(8,128)}), f32[32,80,128]{2,1,0:T(8,128)}, u32[]{:S(2)}, u32[]{:S(2)}) %all-to-all-start) | async-done | bytes 1310752 | tf_op jit(solution)/shard_map/all_to_all | solution.py:178
  289.0 26.5 %shard_map.37 = f32[8,80,512]{2,1,0:T(8,128)S(1)} custom-call(s32[4]{0:T(128)S(1)} %pad_add_fusion.refs_0_, f32[32,80,128]{2,1,0:T(8,128)} %all-to-all-done.refs_1_, f32[4,8,5,32,128]{4,3,2,1,0:T(8,128)} %copy-done.2, f32[4,8,5,32,128]{4,3,2,1,0:T(8,128)} %collective-permute-done.12.refs_3_, f32[4,8,5,32,128]{4,3,2,1,0:T(8,128)} %collective-permute-done.13.refs_4_, ...), custom_call_target="tpu_custom_call" | custom-call | flops 16000000000 | bytes 40000000 | tf_op jit(solution)/shard_map/pallas_call | solution.py:151
  315.5 20.6 %all_to_all.16 = f32[8,80,512]{2,1,0:T(8,128)S(1)} all-to-all(f32[8,80,512]{2,1,0:T(8,128)S(1)} %shard_map.37), channel_id=1, replica_groups=mesh['pair'=32,'aux'=8] {'aux'}, dimensions={0} | all-to-all | bytes 2621440 | tf_op jit(solution)/shard_map/all_to_all | solution.py:181
  (94 shorter events, 16.6 us)
Async XLA Ops:
  11.1 12.4 %collective-permute-start = (f32[8,32,128]{2,1,0:T(8,128)S(1)}, f32[8,32,128]{2,1,0:T(8,128)S(1)}, u32[]{:S(2)}, u32[]{:S(2)}) collective-permute-start(f32[8,32,128]{2,1,0:T(8,128)S(1)} %slice_bitcast_fusion), channel_id=1, source_target_pairs={{0,248},{8,240},{16,232},{24,224},{32,216},{40,208},{48,200},{56,1... | collective-permute-start | bytes 393224 | tf_op jit(solution)/shard_map/ppermute | solution.py:53
  23.7 45.1 %collective-permute-start.7 = (f32[9,32,128]{2,1,0:T(8,128)S(1)}, f32[9,32,128]{2,1,0:T(8,128)S(1)}, u32[]{:S(2)}, u32[]{:S(2)}) collective-permute-start(f32[9,32,128]{2,1,0:T(8,128)S(1)} %constant_dynamic-update-slice_fusion), channel_id=1, source_target_pairs={{0,52},{8,60},{4,0},{12,8},{16,4},{24,12},{20,16},{28,24},{32,20},... | collective-permute-start | bytes 442376 | tf_op jit(solution)/shard_map/ppermute | solution.py:29
  24.1 44.6 %collective-permute-start.6 = (f32[9,32,128]{2,1,0:T(8,128)S(1)}, f32[9,32,128]{2,1,0:T(8,128)S(1)}, u32[]{:S(2)}, u32[]{:S(2)}) collective-permute-start(f32[9,32,128]{2,1,0:T(8,128)S(1)} %constant_dynamic-update-slice_fusion), channel_id=1, source_target_pairs={{0,48},{8,56},{4,52},{12,60},{16,0},{24,8},{20,4},{28,12},{32,16},... | collective-permute-start | bytes 442376 | tf_op jit(solution)/shard_map/ppermute | solution.py:29
  29.3 39.5 %collective-permute-start.5 = (f32[9,32,128]{2,1,0:T(8,128)S(1)}, f32[9,32,128]{2,1,0:T(8,128)S(1)}, u32[]{:S(2)}, u32[]{:S(2)}) collective-permute-start(f32[9,32,128]{2,1,0:T(8,128)S(1)} %constant_dynamic-update-slice_fusion), channel_id=1, source_target_pairs={{0,36},{8,44},{4,48},{12,56},{16,52},{24,60},{20,0},{28,8},{32,4},... | collective-permute-start | bytes 442376 | tf_op jit(solution)/shard_map/ppermute | solution.py:29
  29.8 39.0 %collective-permute-start.4 = (f32[9,32,128]{2,1,0:T(8,128)S(1)}, f32[9,32,128]{2,1,0:T(8,128)S(1)}, u32[]{:S(2)}, u32[]{:S(2)}) collective-permute-start(f32[9,32,128]{2,1,0:T(8,128)S(1)} %constant_dynamic-update-slice_fusion), channel_id=1, source_target_pairs={{0,32},{8,40},{4,36},{12,44},{16,48},{24,56},{20,52},{28,60},{32,0... | collective-permute-start | bytes 442376 | tf_op jit(solution)/shard_map/ppermute | solution.py:29
  32.1 12.4 %collective-permute-start.1 = (f32[9,32,128]{2,1,0:T(8,128)S(1)}, f32[9,32,128]{2,1,0:T(8,128)S(1)}, u32[]{:S(2)}, u32[]{:S(2)}) collective-permute-start(f32[9,32,128]{2,1,0:T(8,128)S(1)} %constant_dynamic-update-slice_fusion), channel_id=1, source_target_pairs={{0,4},{8,12},{4,16},{12,24},{16,20},{24,28},{20,32},{28,40},{32,36... | collective-permute-start | bytes 442376 | tf_op jit(solution)/shard_map/ppermute | solution.py:29
  44.5 10.2 %collective-permute-start.2 = (f32[9,32,128]{2,1,0:T(8,128)S(1)}, f32[9,32,128]{2,1,0:T(8,128)S(1)}, u32[]{:S(2)}, u32[]{:S(2)}) collective-permute-start(f32[9,32,128]{2,1,0:T(8,128)S(1)} %constant_dynamic-update-slice_fusion), channel_id=1, source_target_pairs={{0,16},{8,24},{4,20},{12,28},{16,32},{24,40},{20,36},{28,44},{32,4... | collective-permute-start | bytes 442376 | tf_op jit(solution)/shard_map/ppermute | solution.py:29
  54.7 14.0 %collective-permute-start.3 = (f32[9,32,128]{2,1,0:T(8,128)S(1)}, f32[9,32,128]{2,1,0:T(8,128)S(1)}, u32[]{:S(2)}, u32[]{:S(2)}) collective-permute-start(f32[9,32,128]{2,1,0:T(8,128)S(1)} %constant_dynamic-update-slice_fusion), channel_id=1, source_target_pairs={{0,20},{8,28},{4,32},{12,40},{16,36},{24,44},{20,48},{28,56},{32,5... | collective-permute-start | bytes 442376 | tf_op jit(solution)/shard_map/ppermute | solution.py:29
  68.9 13.9 %collective-permute-start.21 = (f32[8,4,32,128]{3,2,1,0:T(8,128)S(1)}, f32[8,4,32,128]{3,2,1,0:T(8,128)S(1)}, u32[]{:S(2)}, u32[]{:S(2)}) collective-permute-start(f32[8,4,32,128]{3,2,1,0:T(8,128)S(1)} %get-tuple-element.6), channel_id=1, source_target_pairs={{0,1},{8,9},{4,5},{12,13},{16,17},{24,25},{20,21},{28,29},{32,33},... | collective-permute-start | bytes 1572872 | tf_op jit(solution)/shard_map/ppermute | solution.py:29
  71.8 14.9 %collective-permute-start.22 = (f32[8,4,32,128]{3,2,1,0:T(8,128)S(1)}, f32[8,4,32,128]{3,2,1,0:T(8,128)S(1)}, u32[]{:S(2)}, u32[]{:S(2)}) collective-permute-start(f32[8,4,32,128]{3,2,1,0:T(8,128)S(1)} %get-tuple-element.6), channel_id=1, source_target_pairs={{0,3},{8,11},{4,7},{12,15},{16,19},{24,27},{20,23},{28,31},{32,35}... | collective-permute-start | bytes 1572872 | tf_op jit(solution)/shard_map/ppermute | solution.py:29
  86.9 16.9 %collective-permute-start.8 = (f32[8,5,32,128]{3,2,1,0:T(8,128)S(1)}, f32[8,5,32,128]{3,2,1,0:T(8,128)S(1)}, u32[]{:S(2)}, u32[]{:S(2)}) collective-permute-start(f32[8,5,32,128]{3,2,1,0:T(8,128)S(1)} %get-tuple-element.8), channel_id=1, source_target_pairs={{0,64},{8,72},{4,68},{12,76},{16,80},{24,88},{20,84},{28,92},{32,9... | collective-permute-start | bytes 1966088 | tf_op jit(solution)/shard_map/ppermute | solution.py:29
  87.3 18.1 %collective-permute-start.9 = (f32[8,5,32,128]{3,2,1,0:T(8,128)S(1)}, f32[8,5,32,128]{3,2,1,0:T(8,128)S(1)}, u32[]{:S(2)}, u32[]{:S(2)}) collective-permute-start(f32[8,5,32,128]{3,2,1,0:T(8,128)S(1)} %get-tuple-element.8), channel_id=1, source_target_pairs={{0,192},{8,200},{4,196},{12,204},{16,208},{24,216},{20,212},{28,22... | collective-permute-start | bytes 1966088 | tf_op jit(solution)/shard_map/ppermute | solution.py:29
  95.1 65.6 %collective-permute-start.26 = (f32[4,8,4,32,128]{4,3,2,1,0:T(8,128)S(1)}, f32[4,8,4,32,128]{4,3,2,1,0:T(8,128)}, u32[]{:S(2)}, u32[]{:S(2)}) collective-permute-start(f32[4,8,4,32,128]{4,3,2,1,0:T(8,128)S(1)} %pad_maximum_fusion.1.refs_12_), channel_id=1, source_target_pairs={{0,192},{8,200},{4,196},{12,204},{16,208},{24,216},{20,212},{28,22... | collective-permute-start | bytes 6291464 | tf_op jit(solution)/shard_map/ppermute | solution.py:29
  103.9 9.2 %collective-permute-start.10 = (f32[4,5,32,128]{3,2,1,0:T(8,128)S(1)}, f32[4,5,32,128]{3,2,1,0:T(8,128)S(1)}, u32[]{:S(2)}, u32[]{:S(2)}) collective-permute-start(f32[4,5,32,128]{3,2,1,0:T(8,128)S(1)} %slice.51), channel_id=1, source_target_pairs={{0,64},{8,72},{4,68},{12,76},{16,80},{24,88},{20,84},{28,92},{32,9... | collective-permute-start | bytes 983048 | tf_op jit(solution)/shard_map/ppermute | solution.py:29
  105.4 49.8 %collective-permute-start.11 = (f32[4,5,32,128]{3,2,1,0:T(8,128)S(1)}, f32[4,5,32,128]{3,2,1,0:T(8,128)S(1)}, u32[]{:S(2)}, u32[]{:S(2)}) collective-permute-start(f32[4,5,32,128]{3,2,1,0:T(8,128)S(1)} %slice.52), channel_id=1, source_target_pairs={{0,192},{8,200},{4,196},{12,204},{16,208},{24,216},{20,212},{28,22... | collective-permute-start | bytes 983048 | tf_op jit(solution)/shard_map/ppermute | solution.py:29
  155.6 58.1 %collective-permute-start.13 = (f32[4,8,5,32,128]{4,3,2,1,0:T(8,128)S(1)}, f32[4,8,5,32,128]{4,3,2,1,0:T(8,128)}, u32[]{:S(2)}, u32[]{:S(2)}) collective-permute-start(f32[4,8,5,32,128]{4,3,2,1,0:T(8,128)S(1)} %pad_maximum_fusion.refs_2_), channel_id=1, source_target_pairs={{0,3},{8,11},{4,7},{12,15},{16,19},{24,27},{20,23},{28,31},{32,35}... | collective-permute-start | bytes 7864328 | tf_op jit(solution)/shard_map/ppermute | solution.py:29
  155.7 63.4 %collective-permute-start.12 = (f32[4,8,5,32,128]{4,3,2,1,0:T(8,128)S(1)}, f32[4,8,5,32,128]{4,3,2,1,0:T(8,128)}, u32[]{:S(2)}, u32[]{:S(2)}) collective-permute-start(f32[4,8,5,32,128]{4,3,2,1,0:T(8,128)S(1)} %pad_maximum_fusion.refs_2_), channel_id=1, source_target_pairs={{0,1},{8,9},{4,5},{12,13},{16,17},{24,25},{20,21},{28,29},{32,33},... | collective-permute-start | bytes 7864328 | tf_op jit(solution)/shard_map/ppermute | solution.py:29
  158.9 65.9 %collective-permute-start.16 = (f32[4,8,5,32,128]{4,3,2,1,0:T(8,128)S(1)}, f32[4,8,5,32,128]{4,3,2,1,0:T(8,128)S(1)}, u32[]{:S(2)}, u32[]{:S(2)}) collective-permute-start(f32[4,8,5,32,128]{4,3,2,1,0:T(8,128)S(1)} %pad_maximum_fusion.refs_2_), channel_id=1, source_target_pairs={{0,8},{8,0},{4,12},{12,4},{16,24},{24,16},{20,28},{28,20},{32,40},... | collective-permute-start | bytes 7864328 | tf_op jit(solution)/shard_map/ppermute | solution.py:29
  158.9 59.9 %collective-permute-start.25 = (f32[4,8,4,32,128]{4,3,2,1,0:T(8,128)S(1)}, f32[4,8,4,32,128]{4,3,2,1,0:T(8,128)S(1)}, u32[]{:S(2)}, u32[]{:S(2)}) collective-permute-start(f32[4,8,4,32,128]{4,3,2,1,0:T(8,128)S(1)} %pad_maximum_fusion.1.refs_12_), channel_id=1, source_target_pairs={{0,64},{8,72},{4,68},{12,76},{16,80},{24,88},{20,84},{28,92},{32,9... | collective-permute-start | bytes 6291464 | tf_op jit(solution)/shard_map/ppermute | solution.py:29
  160.7 64.0 %collective-permute-start.29 = (f32[4,8,4,32,128]{4,3,2,1,0:T(8,128)S(1)}, f32[4,8,4,32,128]{4,3,2,1,0:T(8,128)S(1)}, u32[]{:S(2)}, u32[]{:S(2)}) collective-permute-start(f32[4,8,4,32,128]{4,3,2,1,0:T(8,128)S(1)} %pad_maximum_fusion.1.refs_12_), channel_id=1, source_target_pairs={{0,8},{8,0},{4,12},{12,4},{16,24},{24,16},{20,28},{28,20},{32,40},... | collective-permute-start | bytes 6291464 | tf_op jit(solution)/shard_map/ppermute | solution.py:29
  213.7 23.4 %collective-permute-start.28 = (f32[2,8,4,32,128]{4,3,2,1,0:T(8,128)S(1)}, f32[2,8,4,32,128]{4,3,2,1,0:T(8,128)S(1)}, u32[]{:S(2)}, u32[]{:S(2)}) collective-permute-start(f32[2,8,4,32,128]{4,3,2,1,0:T(8,128)S(1)} %slice.59), channel_id=1, source_target_pairs={{0,192},{8,200},{4,196},{12,204},{16,208},{24,216},{20,212},{28,22... | collective-permute-start | bytes 3145736 | tf_op jit(solution)/shard_map/ppermute | solution.py:29
  218.8 28.8 %collective-permute-start.15 = (f32[2,8,5,32,128]{4,3,2,1,0:T(8,128)S(1)}, f32[2,8,5,32,128]{4,3,2,1,0:T(8,128)S(1)}, u32[]{:S(2)}, u32[]{:S(2)}) collective-permute-start(f32[2,8,5,32,128]{4,3,2,1,0:T(8,128)S(1)} %slice.54), channel_id=1, source_target_pairs={{0,3},{8,11},{4,7},{12,15},{16,19},{24,27},{20,23},{28,31},{32,35}... | collective-permute-start | bytes 3932168 | tf_op jit(solution)/shard_map/ppermute | solution.py:29
  222.1 31.5 %collective-permute-start.14 = (f32[2,8,5,32,128]{4,3,2,1,0:T(8,128)}, f32[2,8,5,32,128]{4,3,2,1,0:T(8,128)}, u32[]{:S(2)}, u32[]{:S(2)}) collective-permute-start(f32[2,8,5,32,128]{4,3,2,1,0:T(8,128)} %slice.53), channel_id=1, source_target_pairs={{0,1},{8,9},{4,5},{12,13},{16,17},{24,25},{20,21},{28,29},{32,33},... | collective-permute-start | bytes 3932168 | tf_op jit(solution)/shard_map/ppermute | solution.py:29
  224.7 22.5 %collective-permute-start.27 = (f32[2,8,4,32,128]{4,3,2,1,0:T(8,128)S(1)}, f32[2,8,4,32,128]{4,3,2,1,0:T(8,128)S(1)}, u32[]{:S(2)}, u32[]{:S(2)}) collective-permute-start(f32[2,8,4,32,128]{4,3,2,1,0:T(8,128)S(1)} %slice.58), channel_id=1, source_target_pairs={{0,64},{8,72},{4,68},{12,76},{16,80},{24,88},{20,84},{28,92},{32,9... | collective-permute-start | bytes 3145736 | tf_op jit(solution)/shard_map/ppermute | solution.py:29
  224.8 29.4 %collective-permute-start.31 = (f32[4,8,4,32,128]{4,3,2,1,0:T(8,128)}, f32[4,8,4,32,128]{4,3,2,1,0:T(8,128)}, u32[]{:S(2)}, u32[]{:S(2)}) collective-permute-start(f32[4,8,4,32,128]{4,3,2,1,0:T(8,128)} %collective-permute-done.26.refs_14_), channel_id=1, source_target_pairs={{0,8},{8,0},{4,12},{12,4},{16,24},{24,16},{20,28},{28,20},{32,40},... | collective-permute-start | bytes 6291464 | tf_op jit(solution)/shard_map/ppermute | solution.py:29
  237.1 16.7 %collective-permute-start.33 = (f32[2,8,4,32,128]{4,3,2,1,0:T(8,128)S(1)}, f32[2,8,4,32,128]{4,3,2,1,0:T(8,128)S(1)}, u32[]{:S(2)}, u32[]{:S(2)}) collective-permute-start(f32[2,8,4,32,128]{4,3,2,1,0:T(8,128)S(1)} %collective-permute-done.28.refs_16_), channel_id=1, source_target_pairs={{0,8},{8,0},{4,12},{12,4},{16,24},{24,16},{20,28},{28,20},{32,40},... | collective-permute-start | bytes 3145736 | tf_op jit(solution)/shard_map/ppermute | solution.py:29
  247.3 40.5 %collective-permute-start.18 = (f32[4,8,5,32,128]{4,3,2,1,0:T(8,128)}, f32[4,8,5,32,128]{4,3,2,1,0:T(8,128)}, u32[]{:S(2)}, u32[]{:S(2)}) collective-permute-start(f32[4,8,5,32,128]{4,3,2,1,0:T(8,128)} %collective-permute-done.13.refs_4_), channel_id=1, source_target_pairs={{0,8},{8,0},{4,12},{12,4},{16,24},{24,16},{20,28},{28,20},{32,40},... | collective-permute-start | bytes 7864328 | tf_op jit(solution)/shard_map/ppermute | solution.py:29
  248.7 39.0 %collective-permute-start.17 = (f32[4,8,5,32,128]{4,3,2,1,0:T(8,128)}, f32[4,8,5,32,128]{4,3,2,1,0:T(8,128)}, u32[]{:S(2)}, u32[]{:S(2)}) collective-permute-start(f32[4,8,5,32,128]{4,3,2,1,0:T(8,128)} %collective-permute-done.12.refs_3_), channel_id=1, source_target_pairs={{0,8},{8,0},{4,12},{12,4},{16,24},{24,16},{20,28},{28,20},{32,40},... | collective-permute-start | bytes 7864328 | tf_op jit(solution)/shard_map/ppermute | solution.py:29
  248.9 38.8 %all-to-all-start = ((f32[32,80,128]{2,1,0:T(8,128)}), f32[32,80,128]{2,1,0:T(8,128)}, u32[]{:S(2)}, u32[]{:S(2)}) async-start(f32[32,80,128]{2,1,0:T(8,128)} %param.3), calls=%async_computation | async-start | bytes 2621440 | tf_op jit(solution)/shard_map/all_to_all | solution.py:178
  253.8 33.9 %collective-permute-start.30 = (f32[4,8,4,32,128]{4,3,2,1,0:T(8,128)}, f32[4,8,4,32,128]{4,3,2,1,0:T(8,128)}, u32[]{:S(2)}, u32[]{:S(2)}) collective-permute-start(f32[4,8,4,32,128]{4,3,2,1,0:T(8,128)} %copy-done.4), channel_id=1, source_target_pairs={{0,8},{8,0},{4,12},{12,4},{16,24},{24,16},{20,28},{28,20},{32,40},... | collective-permute-start | bytes 6291464 | tf_op jit(solution)/shard_map/ppermute | solution.py:29
  254.2 33.5 %collective-permute-start.20 = (f32[2,8,5,32,128]{4,3,2,1,0:T(8,128)}, f32[2,8,5,32,128]{4,3,2,1,0:T(8,128)}, u32[]{:S(2)}, u32[]{:S(2)}) collective-permute-start(f32[2,8,5,32,128]{4,3,2,1,0:T(8,128)} %copy-done.7), channel_id=1, source_target_pairs={{0,8},{8,0},{4,12},{12,4},{16,24},{24,16},{20,28},{28,20},{32,40},... | collective-permute-start | bytes 3932168 | tf_op jit(solution)/shard_map/ppermute | solution.py:29
  258.7 29.1 %collective-permute-start.19 = (f32[2,8,5,32,128]{4,3,2,1,0:T(8,128)}, f32[2,8,5,32,128]{4,3,2,1,0:T(8,128)}, u32[]{:S(2)}, u32[]{:S(2)}) collective-permute-start(f32[2,8,5,32,128]{4,3,2,1,0:T(8,128)} %collective-permute-done.14.refs_5_), channel_id=1, source_target_pairs={{0,8},{8,0},{4,12},{12,4},{16,24},{24,16},{20,28},{28,20},{32,40},... | collective-permute-start | bytes 3932168 | tf_op jit(solution)/shard_map/ppermute | solution.py:29
  (11 other events, 201.8 us)

commit v2 on v1

--- a/solution.py
+++ b/solution.py
@@ -33,14 +33,32 @@
     return lambda value, d: shift(value, **{axis: d})
 
 
-def rings(block, first, second):
-    one, two = along(first), along(second)
-    up, down = one(block, 1), one(block, -1)
-    far = jnp.concatenate([one(up[:4], 1), one(down[4:], -1)])
-    whole = jnp.stack([block, up, down, far])
-    up, down = two(whole, 1), two(whole, -1)
-    far_up, far_down = two(up[:2], 1), two(down[2:], -1)
-    return [whole, up, down, far_up, far_down]
+def ring_of_eight(piece):
+    up, down = [piece], [piece]
+    for _ in range(3):
+        up.append(shift(up[-1], dz=1))
+        down.append(shift(down[-1], dz=-1))
+    far = jnp.concatenate([shift(up[3][:EARLY], dz=1), shift(down[3][EARLY:], dz=-1)])
+    return jnp.stack(up + [far] + down[:0:-1])
+
+
+def gather(column, integrals):
+    blocks = [column[:, :EARLY], column[:, EARLY:]]
+    first = [along("dx"), along("dy")]
+    second = [along("dy"), along("dx")]
+    near = [(one(block, 1), one(block, -1)) for one, block in zip(first, blocks)]
+    near = lax.optimization_barrier(near)
+    far = [(one(up[:4], 1), one(down[4:], -1)) for one, (up, down) in zip(first, near)]
+    whole = [
+        jnp.stack([block, up, down, jnp.concatenate(ends)])
+        for block, (up, down), ends in zip(blocks, near, far)
+    ]
+    whole, integrals = lax.optimization_barrier((whole, integrals))
+    near = [(two(block, 1), two(block, -1)) for two, block in zip(second, whole)]
+    rows = lax.all_to_all(integrals, "pair", 0, 0, tiled=True)
+    near, rows = lax.optimization_barrier((near, rows))
+    far = [(two(up[:2], 1), two(down[2:], -1)) for two, (up, down) in zip(second, near)]
+    return rows, [[block, *sides, *ends] for block, sides, ends in zip(whole, near, far)]
 
 
 def pieces(factor, diag_inverse, pair, aux):
@@ -172,10 +190,7 @@
     place = jnp.stack([x, aux % NY, z, core]).astype(jnp.int32)
 
     piece = pieces(factor, diag_inverse, pair, aux)
-    column = jnp.stack([piece] + [shift(piece, dz=d) for d in range(1, NZ)])
-    early = rings(column[:, :EARLY], "dx", "dy")
-    late = rings(column[:, EARLY:], "dy", "dx")
-    rows = lax.all_to_all(integrals, "pair", 0, 0, tiled=True)
+    rows, (early, late) = gather(ring_of_eight(piece), integrals)
     arrays = early + [shift(v, core=1) for v in early] + late + [shift(v, core=1) for v in late]
     solved = solve(place, rows, arrays)
     result = lax.all_to_all(solved, "aux", 0, 0, tiled=True)

time: 340 us -> 259 us (0.76)
  waiting for transfers between devices: 215 us -> 138 us
  starting transfers between devices: 52.5 us -> 46.7 us
    ppermute x33 -> x34, waiting for transfers between devices: 179 us -> 131 us  [shift(): return lax.ppermute(value, ALL, pairs)]
    all_to_all x1, waiting for transfers between devices: 28.8 us -> 0.01 us  [gather(): rows = lax.all_to_all(integrals, 'pair', 0, 0, tiled=True)]
    ppermute x33 -> x34, starting transfers between devices: 42.1 us -> 33.6 us  [shift(): return lax.ppermute(value, ALL, pairs)]
  transfers between devices with their start and end apart: 35 -> 36, of which waited for: 17 -> 22; matrix products, arithmetic and copies ran while one was open for 2% -> 2% of each run, Pallas kernels for 0% -> 0%
where the time goes in v2:
time: 259 us; the launch traced here: 257 us
  waiting for transfers between devices  138 us (53%)
  starting transfers between devices  46.7 us (18%)
  blocking collectives  32.8 us (13%)
  Pallas kernels  26.5 us (10%)
  local copies, waits for them, and re-layouts  9.12 us (4%)
  other arithmetic  3.32 us (1%)
    ppermute x34, waiting for transfers between devices, shift(): return lax.ppermute(value, ALL, pairs)  131 us
    ppermute x34, starting transfers between devices, shift(): return lax.ppermute(value, ALL, pairs)  33.6 us
    pallas_call x1, Pallas kernels, solve(): pl.pallas_call(kernel, out_shape=jax.ShapeDtypeStruct((PANELS, ROWS, PANE...  26.5 us
    all_to_all x1, blocking collectives, local(): result = lax.all_to_all(solved, 'aux', 0, 0, tiled=True)  22.8 us
    all_to_all x1, blocking collectives, pieces(): chunks = lax.all_to_all(chunks, 'aux', 0, 0, tiled=True)  10 us
    all_to_all x1, starting transfers between devices, gather(): rows = lax.all_to_all(integrals, 'pair', 0, 0, tiled=True)  7.4 us
    ppermute x1, waiting for transfers between devices, pieces(): other = lax.ppermute(chunks[:, 1], 'pair', [(p, 31 - p) for p in range(32)])  6.69 us
    ppermute x1, starting transfers between devices, pieces(): other = lax.ppermute(chunks[:, 1], 'pair', [(p, 31 - p) for p in range(32)])  5.69 us
  transfers between devices with their start and end apart: 36, of which 22 were waited for; matrix products, arithmetic and copies ran while one was open for 2% of the time, Pallas kernels for 0%

profile of v2, /device:TPU:56, one launch (start us, length us, event | category | flops | bytes accessed | tf_op | source)
XLA Modules:
  0.0 256.7 jit_solution(12923721794981739596)
XLA Ops:
  1.1 10.0 %all_to_all.15 = f32[8,2,32,128]{3,2,1,0:T(8,128)S(1)} all-to-all(f32[8,2,32,128]{3,2,1,0:T(8,128)S(1)} %copy.6), channel_id=1, replica_groups=mesh['pair'=32,'aux'=8] {'aux'}, dimensions={0} | all-to-all | bytes 524288 | tf_op jit(solution)/shard_map/all_to_all | solution.py:69
  11.1 5.7 %collective-permute-start = (f32[8,32,128]{2,1,0:T(8,128)S(1)}, f32[8,32,128]{2,1,0:T(8,128)S(1)}, u32[]{:S(2)}, u32[]{:S(2)}) collective-permute-start(f32[8,32,128]{2,1,0:T(8,128)S(1)} %slice_bitcast_fusion), channel_id=1, source_target_pairs={{0,248},{8,240},{16,232},{24,224},{32,216},{40,208},{48,200},{56,1... | collective-permute-start | bytes 393224 | tf_op jit(solution)/shard_map/ppermute | solution.py:71
  16.8 6.7 %collective-permute-done = f32[8,32,128]{2,1,0:T(8,128)S(1)} collective-permute-done((f32[8,32,128]{2,1,0:T(8,128)S(1)}, f32[8,32,128]{2,1,0:T(8,128)S(1)}, u32[]{:S(2)}, u32[]{:S(2)}) %collective-permute-start) | collective-permute-done | bytes 131104 | tf_op jit(solution)/shard_map/ppermute | solution.py:71
  24.1 2.7 %collective-permute-start.1 = (f32[9,32,128]{2,1,0:T(8,128)S(1)}, f32[9,32,128]{2,1,0:T(8,128)S(1)}, u32[]{:S(2)}, u32[]{:S(2)}) collective-permute-start(f32[9,32,128]{2,1,0:T(8,128)S(1)} %constant_dynamic-update-slice_fusion), channel_id=1, source_target_pairs={{0,4},{8,12},{4,16},{12,24},{16,20},{24,28},{20,32},{28,40},{32,36... | collective-permute-start | bytes 442376 | tf_op jit(solution)/shard_map/ppermute | solution.py:29
  26.9 4.0 %collective-permute-done.5 = f32[9,32,128]{2,1,0:T(8,128)S(1)} collective-permute-done((f32[9,32,128]{2,1,0:T(8,128)S(1)}, f32[9,32,128]{2,1,0:T(8,128)S(1)}, u32[]{:S(2)}, u32[]{:S(2)}) %collective-permute-start.5) | collective-permute-done | bytes 147488 | tf_op jit(solution)/shard_map/ppermute | solution.py:29
  30.9 2.0 collective-permute-start.2
  32.9 3.2 %collective-permute-done.6 = f32[9,32,128]{2,1,0:T(8,128)S(1)} collective-permute-done((f32[9,32,128]{2,1,0:T(8,128)S(1)}, f32[9,32,128]{2,1,0:T(8,128)S(1)}, u32[]{:S(2)}, u32[]{:S(2)}) %collective-permute-start.6) | collective-permute-done | bytes 147488 | tf_op jit(solution)/shard_map/ppermute | solution.py:29
  36.5 1.7 collective-permute-start.3
  38.2 3.1 %collective-permute-done.7 = f32[9,32,128]{2,1,0:T(8,128)S(1)} collective-permute-done((f32[9,32,128]{2,1,0:T(8,128)S(1)}, f32[9,32,128]{2,1,0:T(8,128)S(1)}, u32[]{:S(2)}, u32[]{:S(2)}) %collective-permute-start.7) | collective-permute-done | bytes 147488 | tf_op jit(solution)/shard_map/ppermute | solution.py:29
  43.5 2.1 collective-permute-done.8
  45.6 2.6 %collective-permute-done.4 = f32[5,32,128]{2,1,0:T(8,128)S(1)} collective-permute-done((f32[5,32,128]{2,1,0:T(8,128)S(1)}, f32[5,32,128]{2,1,0:T(8,128)S(1)}, u32[]{:S(2)}, u32[]{:S(2)}) %collective-permute-start.4) | collective-permute-done | bytes 81952 | tf_op jit(solution)/shard_map/ppermute | solution.py:29
  48.7 3.0 %collective-permute-start.10 = (f32[8,5,32,128]{3,2,1,0:T(8,128)S(1)}, f32[8,5,32,128]{3,2,1,0:T(8,128)S(1)}, u32[]{:S(2)}, u32[]{:S(2)}) collective-permute-start(f32[8,5,32,128]{3,2,1,0:T(8,128)S(1)} %get-tuple-element.32), channel_id=1, source_target_pairs={{0,192},{8,200},{4,196},{12,204},{16,208},{24,216},{20,212},{28,22... | collective-permute-start | bytes 1966088 | tf_op jit(solution)/shard_map/ppermute | solution.py:29
  52.9 2.2 collective-permute-start.11
  55.1 8.4 %collective-permute-done.12 = f32[8,4,32,128]{3,2,1,0:T(8,128)S(1)} collective-permute-done((f32[8,4,32,128]{3,2,1,0:T(8,128)S(1)}, f32[8,4,32,128]{3,2,1,0:T(8,128)S(1)}, u32[]{:S(2)}, u32[]{:S(2)}) %collective-permute-start.12) | collective-permute-done | bytes 524320 | tf_op jit(solution)/shard_map/ppermute | solution.py:29
  64.6 2.6 %collective-permute-start.15 = (f32[4,4,32,128]{3,2,1,0:T(8,128)S(1)}, f32[4,4,32,128]{3,2,1,0:T(8,128)S(1)}, u32[]{:S(2)}, u32[]{:S(2)}) collective-permute-start(f32[4,4,32,128]{3,2,1,0:T(8,128)S(1)} %slice.50), channel_id=1, source_target_pairs={{0,1},{8,9},{4,5},{12,13},{16,17},{24,25},{20,21},{28,29},{32,33},... | collective-permute-start | bytes 786440 | tf_op jit(solution)/shard_map/ppermute | solution.py:29
  69.5 1.9 collective-permute-done.16
  71.7 2.9 %collective-permute-done.14 = f32[4,5,32,128]{3,2,1,0:T(8,128)S(1)} collective-permute-done((f32[4,5,32,128]{3,2,1,0:T(8,128)S(1)}, f32[4,5,32,128]{3,2,1,0:T(8,128)S(1)}, u32[]{:S(2)}, u32[]{:S(2)}) %collective-permute-start.14) | collective-permute-done | bytes 327712 | tf_op jit(solution)/shard_map/ppermute | solution.py:29
  74.6 2.2 collective-permute-done.13
  76.8 1.7 pad_maximum_fusion.refs_2_
  80.1 2.4 collective-permute-start.17
  82.5 7.4 %all-to-all-start.1 = ((f32[32,80,128]{2,1,0:T(8,128)}), f32[32,80,128]{2,1,0:T(8,128)}, u32[]{:S(2)}, u32[]{:S(2)}) async-start(f32[32,80,128]{2,1,0:T(8,128)} %param.3), calls=%async_computation.1 | async-start | bytes 2621440 | tf_op jit(solution)/shard_map/all_to_all | solution.py:58
  89.9 1.8 collective-permute-start.19
  91.7 40.2 %collective-permute-done.20.refs_14_ = f32[4,8,4,32,128]{4,3,2,1,0:T(8,128)} collective-permute-done((f32[4,8,4,32,128]{4,3,2,1,0:T(8,128)S(1)}, f32[4,8,4,32,128]{4,3,2,1,0:T(8,128)}, u32[]{:S(2)}, u32[]{:S(2)}) %collective-permute-start.20) | collective-permute-done | bytes 2097184 | tf_op jit(solution)/shard_map/ppermute | solution.py:29
  131.9 21.1 %collective-permute-done.19.refs_13_ = f32[4,8,4,32,128]{4,3,2,1,0:T(8,128)} collective-permute-done((f32[4,8,4,32,128]{4,3,2,1,0:T(8,128)S(1)}, f32[4,8,4,32,128]{4,3,2,1,0:T(8,128)}, u32[]{:S(2)}, u32[]{:S(2)}) %collective-permute-start.19) | collective-permute-done | bytes 2097184 | tf_op jit(solution)/shard_map/ppermute | solution.py:29
  158.2 3.3 %collective-permute-start.21 = (f32[2,8,5,32,128]{4,3,2,1,0:T(8,128)S(1)}, f32[2,8,5,32,128]{4,3,2,1,0:T(8,128)}, u32[]{:S(2)}, u32[]{:S(2)}) collective-permute-start(f32[2,8,5,32,128]{4,3,2,1,0:T(8,128)S(1)} %slice.52), channel_id=1, source_target_pairs={{0,1},{8,9},{4,5},{12,13},{16,17},{24,25},{20,21},{28,29},{32,33},... | collective-permute-start | bytes 3932168 | tf_op jit(solution)/shard_map/ppermute | solution.py:29
  164.1 14.9 %collective-permute-done.29.refs_16_ = f32[2,8,4,32,128]{4,3,2,1,0:T(8,128)S(1)} collective-permute-done((f32[2,8,4,32,128]{4,3,2,1,0:T(8,128)S(1)}, f32[2,8,4,32,128]{4,3,2,1,0:T(8,128)S(1)}, u32[]{:S(2)}, u32[]{:S(2)}) %collective-permute-start.29) | collective-permute-done | bytes 1048608 | tf_op jit(solution)/shard_map/ppermute | solution.py:29
  179.0 8.8 %collective-permute-done.28.refs_15_ = f32[2,8,4,32,128]{4,3,2,1,0:T(8,128)S(1)} collective-permute-done((f32[2,8,4,32,128]{4,3,2,1,0:T(8,128)S(1)}, f32[2,8,4,32,128]{4,3,2,1,0:T(8,128)S(1)}, u32[]{:S(2)}, u32[]{:S(2)}) %collective-permute-start.28) | collective-permute-done | bytes 1048608 | tf_op jit(solution)/shard_map/ppermute | solution.py:29
  189.2 9.1 %collective-permute-done.33.refs_20_ = f32[2,8,4,32,128]{4,3,2,1,0:T(8,128)S(1)} collective-permute-done((f32[2,8,4,32,128]{4,3,2,1,0:T(8,128)S(1)}, f32[2,8,4,32,128]{4,3,2,1,0:T(8,128)S(1)}, u32[]{:S(2)}, u32[]{:S(2)}) %collective-permute-start.33) | collective-permute-done | bytes 1048608 | tf_op jit(solution)/shard_map/ppermute | solution.py:29
  201.3 1.9 collective-permute-done.27.refs_11_
  203.2 1.9 collective-permute-done.26.refs_10_
  206.3 26.5 %shard_map.37 = f32[8,80,512]{2,1,0:T(8,128)S(1)} custom-call(s32[4]{0:T(128)S(1)} %pad_add_fusion.refs_0_, f32[32,80,128]{2,1,0:T(8,128)} %all-to-all-done.1.refs_1_, f32[4,8,5,32,128]{4,3,2,1,0:T(8,128)} %pad_maximum_fusion.refs_2_, f32[4,8,5,32,128]{4,3,2,1,0:T(8,128)} %collective-permute-done.17.refs_3_, ...), custom_call_target="tpu_custom_call" | custom-call | flops 16000000000 | bytes 40000000 | tf_op jit(solution)/shard_map/pallas_call | solution.py:169
  232.8 22.8 %all_to_all.16 = f32[8,80,512]{2,1,0:T(8,128)S(1)} all-to-all(f32[8,80,512]{2,1,0:T(8,128)S(1)} %shard_map.37), channel_id=1, replica_groups=mesh['pair'=32,'aux'=8] {'aux'}, dimensions={0} | all-to-all | bytes 2621440 | tf_op jit(solution)/shard_map/all_to_all | solution.py:196
  (88 shorter events, 25.6 us)
Async XLA Ops:
  11.1 12.4 %collective-permute-start = (f32[8,32,128]{2,1,0:T(8,128)S(1)}, f32[8,32,128]{2,1,0:T(8,128)S(1)}, u32[]{:S(2)}, u32[]{:S(2)}) collective-permute-start(f32[8,32,128]{2,1,0:T(8,128)S(1)} %slice_bitcast_fusion), channel_id=1, source_target_pairs={{0,248},{8,240},{16,232},{24,224},{32,216},{40,208},{48,200},{56,1... | collective-permute-start | bytes 393224 | tf_op jit(solution)/shard_map/ppermute | solution.py:71
  23.7 7.2 %collective-permute-start.5 = (f32[9,32,128]{2,1,0:T(8,128)S(1)}, f32[9,32,128]{2,1,0:T(8,128)S(1)}, u32[]{:S(2)}, u32[]{:S(2)}) collective-permute-start(f32[9,32,128]{2,1,0:T(8,128)S(1)} %constant_dynamic-update-slice_fusion), channel_id=1, source_target_pairs={{0,52},{8,60},{4,0},{12,8},{16,4},{24,12},{20,16},{28,24},{32,20},... | collective-permute-start | bytes 442376 | tf_op jit(solution)/shard_map/ppermute | solution.py:29
  24.1 6.8 %collective-permute-start.1 = (f32[9,32,128]{2,1,0:T(8,128)S(1)}, f32[9,32,128]{2,1,0:T(8,128)S(1)}, u32[]{:S(2)}, u32[]{:S(2)}) collective-permute-start(f32[9,32,128]{2,1,0:T(8,128)S(1)} %constant_dynamic-update-slice_fusion), channel_id=1, source_target_pairs={{0,4},{8,12},{4,16},{12,24},{16,20},{24,28},{20,32},{28,40},{32,36... | collective-permute-start | bytes 442376 | tf_op jit(solution)/shard_map/ppermute | solution.py:29
  30.9 5.6 %collective-permute-start.2 = (f32[9,32,128]{2,1,0:T(8,128)S(1)}, f32[9,32,128]{2,1,0:T(8,128)S(1)}, u32[]{:S(2)}, u32[]{:S(2)}) collective-permute-start(f32[9,32,128]{2,1,0:T(8,128)S(1)} %collective-permute-done.1), channel_id=1, source_target_pairs={{0,4},{8,12},{4,16},{12,24},{16,20},{24,28},{20,32},{28,40},{32,36... | collective-permute-start | bytes 442376 | tf_op jit(solution)/shard_map/ppermute | solution.py:29
  36.5 6.1 %collective-permute-start.3 = (f32[9,32,128]{2,1,0:T(8,128)S(1)}, f32[9,32,128]{2,1,0:T(8,128)S(1)}, u32[]{:S(2)}, u32[]{:S(2)}) collective-permute-start(f32[9,32,128]{2,1,0:T(8,128)S(1)} %collective-permute-done.2), channel_id=1, source_target_pairs={{0,4},{8,12},{4,16},{12,24},{16,20},{24,28},{20,32},{28,40},{32,36... | collective-permute-start | bytes 442376 | tf_op jit(solution)/shard_map/ppermute | solution.py:29
  42.5 5.7 %collective-permute-start.4 = (f32[5,32,128]{2,1,0:T(8,128)S(1)}, f32[5,32,128]{2,1,0:T(8,128)S(1)}, u32[]{:S(2)}, u32[]{:S(2)}) collective-permute-start(f32[5,32,128]{2,1,0:T(8,128)S(1)} %slice.58), channel_id=1, source_target_pairs={{0,4},{8,12},{4,16},{12,24},{16,20},{24,28},{20,32},{28,40},{32,36... | collective-permute-start | bytes 245768 | tf_op jit(solution)/shard_map/ppermute | solution.py:29
  48.4 15.2 %collective-permute-start.9 = (f32[8,5,32,128]{3,2,1,0:T(8,128)S(1)}, f32[8,5,32,128]{3,2,1,0:T(8,128)S(1)}, u32[]{:S(2)}, u32[]{:S(2)}) collective-permute-start(f32[8,5,32,128]{3,2,1,0:T(8,128)S(1)} %get-tuple-element.32), channel_id=1, source_target_pairs={{0,64},{8,72},{4,68},{12,76},{16,80},{24,88},{20,84},{28,92},{32,9... | collective-permute-start | bytes 1966088 | tf_op jit(solution)/shard_map/ppermute | solution.py:29
  48.7 14.9 %collective-permute-start.10 = (f32[8,5,32,128]{3,2,1,0:T(8,128)S(1)}, f32[8,5,32,128]{3,2,1,0:T(8,128)S(1)}, u32[]{:S(2)}, u32[]{:S(2)}) collective-permute-start(f32[8,5,32,128]{3,2,1,0:T(8,128)S(1)} %get-tuple-element.32), channel_id=1, source_target_pairs={{0,192},{8,200},{4,196},{12,204},{16,208},{24,216},{20,212},{28,22... | collective-permute-start | bytes 1966088 | tf_op jit(solution)/shard_map/ppermute | solution.py:29
  51.8 11.7 %collective-permute-start.12 = (f32[8,4,32,128]{3,2,1,0:T(8,128)S(1)}, f32[8,4,32,128]{3,2,1,0:T(8,128)S(1)}, u32[]{:S(2)}, u32[]{:S(2)}) collective-permute-start(f32[8,4,32,128]{3,2,1,0:T(8,128)S(1)} %get-tuple-element.30), channel_id=1, source_target_pairs={{0,3},{8,11},{4,7},{12,15},{16,19},{24,27},{20,23},{28,31},{32,35}... | collective-permute-start | bytes 1572872 | tf_op jit(solution)/shard_map/ppermute | solution.py:29
  52.9 10.7 %collective-permute-start.11 = (f32[8,4,32,128]{3,2,1,0:T(8,128)S(1)}, f32[8,4,32,128]{3,2,1,0:T(8,128)S(1)}, u32[]{:S(2)}, u32[]{:S(2)}) collective-permute-start(f32[8,4,32,128]{3,2,1,0:T(8,128)S(1)} %get-tuple-element.30), channel_id=1, source_target_pairs={{0,1},{8,9},{4,5},{12,13},{16,17},{24,25},{20,21},{28,29},{32,33},... | collective-permute-start | bytes 1572872 | tf_op jit(solution)/shard_map/ppermute | solution.py:29
  63.6 7.8 %collective-permute-start.16 = (f32[4,4,32,128]{3,2,1,0:T(8,128)S(1)}, f32[4,4,32,128]{3,2,1,0:T(8,128)S(1)}, u32[]{:S(2)}, u32[]{:S(2)}) collective-permute-start(f32[4,4,32,128]{3,2,1,0:T(8,128)S(1)} %slice.51), channel_id=1, source_target_pairs={{0,3},{8,11},{4,7},{12,15},{16,19},{24,27},{20,23},{28,31},{32,35}... | collective-permute-start | bytes 786440 | tf_op jit(solution)/shard_map/ppermute | solution.py:29
  64.6 6.8 %collective-permute-start.15 = (f32[4,4,32,128]{3,2,1,0:T(8,128)S(1)}, f32[4,4,32,128]{3,2,1,0:T(8,128)S(1)}, u32[]{:S(2)}, u32[]{:S(2)}) collective-permute-start(f32[4,4,32,128]{3,2,1,0:T(8,128)S(1)} %slice.50), channel_id=1, source_target_pairs={{0,1},{8,9},{4,5},{12,13},{16,17},{24,25},{20,21},{28,29},{32,33},... | collective-permute-start | bytes 786440 | tf_op jit(solution)/shard_map/ppermute | solution.py:29
  67.2 7.4 %collective-permute-start.14 = (f32[4,5,32,128]{3,2,1,0:T(8,128)S(1)}, f32[4,5,32,128]{3,2,1,0:T(8,128)S(1)}, u32[]{:S(2)}, u32[]{:S(2)}) collective-permute-start(f32[4,5,32,128]{3,2,1,0:T(8,128)S(1)} %slice.49), channel_id=1, source_target_pairs={{0,192},{8,200},{4,196},{12,204},{16,208},{24,216},{20,212},{28,22... | collective-permute-start | bytes 983048 | tf_op jit(solution)/shard_map/ppermute | solution.py:29
  68.5 8.3 %collective-permute-start.13 = (f32[4,5,32,128]{3,2,1,0:T(8,128)S(1)}, f32[4,5,32,128]{3,2,1,0:T(8,128)S(1)}, u32[]{:S(2)}, u32[]{:S(2)}) collective-permute-start(f32[4,5,32,128]{3,2,1,0:T(8,128)S(1)} %slice.48), channel_id=1, source_target_pairs={{0,64},{8,72},{4,68},{12,76},{16,80},{24,88},{20,84},{28,92},{32,9... | collective-permute-start | bytes 983048 | tf_op jit(solution)/shard_map/ppermute | solution.py:29
  78.5 53.4 %collective-permute-start.20 = (f32[4,8,4,32,128]{4,3,2,1,0:T(8,128)S(1)}, f32[4,8,4,32,128]{4,3,2,1,0:T(8,128)}, u32[]{:S(2)}, u32[]{:S(2)}) collective-permute-start(f32[4,8,4,32,128]{4,3,2,1,0:T(8,128)S(1)} %pad_maximum_fusion.1.refs_12_), channel_id=1, source_target_pairs={{0,192},{8,200},{4,196},{12,204},{16,208},{24,216},{20,212},{28,22... | collective-permute-start | bytes 6291464 | tf_op jit(solution)/shard_map/ppermute | solution.py:29
  79.3 73.7 %collective-permute-start.18 = (f32[4,8,5,32,128]{4,3,2,1,0:T(8,128)}, f32[4,8,5,32,128]{4,3,2,1,0:T(8,128)}, u32[]{:S(2)}, u32[]{:S(2)}) collective-permute-start(f32[4,8,5,32,128]{4,3,2,1,0:T(8,128)} %pad_maximum_fusion.refs_2_), channel_id=1, source_target_pairs={{0,3},{8,11},{4,7},{12,15},{16,19},{24,27},{20,23},{28,31},{32,35}... | collective-permute-start | bytes 7864328 | tf_op jit(solution)/shard_map/ppermute | solution.py:29
  80.1 72.9 %collective-permute-start.17 = (f32[4,8,5,32,128]{4,3,2,1,0:T(8,128)}, f32[4,8,5,32,128]{4,3,2,1,0:T(8,128)}, u32[]{:S(2)}, u32[]{:S(2)}) collective-permute-start(f32[4,8,5,32,128]{4,3,2,1,0:T(8,128)} %pad_maximum_fusion.refs_2_), channel_id=1, source_target_pairs={{0,1},{8,9},{4,5},{12,13},{16,17},{24,25},{20,21},{28,29},{32,33},... | collective-permute-start | bytes 7864328 | tf_op jit(solution)/shard_map/ppermute | solution.py:29
  82.5 70.5 %all-to-all-start.1 = ((f32[32,80,128]{2,1,0:T(8,128)}), f32[32,80,128]{2,1,0:T(8,128)}, u32[]{:S(2)}, u32[]{:S(2)}) async-start(f32[32,80,128]{2,1,0:T(8,128)} %param.3), calls=%async_computation.1 | async-start | bytes 2621440 | tf_op jit(solution)/shard_map/all_to_all | solution.py:58
  89.9 63.1 %collective-permute-start.19 = (f32[4,8,4,32,128]{4,3,2,1,0:T(8,128)S(1)}, f32[4,8,4,32,128]{4,3,2,1,0:T(8,128)}, u32[]{:S(2)}, u32[]{:S(2)}) collective-permute-start(f32[4,8,4,32,128]{4,3,2,1,0:T(8,128)S(1)} %pad_maximum_fusion.1.refs_12_), channel_id=1, source_target_pairs={{0,64},{8,72},{4,68},{12,76},{16,80},{24,88},{20,84},{28,92},{32,9... | collective-permute-start | bytes 6291464 | tf_op jit(solution)/shard_map/ppermute | solution.py:29
  91.7 72.4 %collective-permute-start.23 = (f32[4,8,5,32,128]{4,3,2,1,0:T(8,128)}, f32[4,8,5,32,128]{4,3,2,1,0:T(8,128)}, u32[]{:S(2)}, u32[]{:S(2)}) collective-permute-start(f32[4,8,5,32,128]{4,3,2,1,0:T(8,128)} %pad_maximum_fusion.refs_2_), channel_id=1, source_target_pairs={{0,8},{8,0},{4,12},{12,4},{16,24},{24,16},{20,28},{28,20},{32,40},... | collective-permute-start | bytes 7864328 | tf_op jit(solution)/shard_map/ppermute | solution.py:29
  131.9 30.9 %collective-permute-start.30 = (f32[4,8,4,32,128]{4,3,2,1,0:T(8,128)S(1)}, f32[4,8,4,32,128]{4,3,2,1,0:T(8,128)}, u32[]{:S(2)}, u32[]{:S(2)}) collective-permute-start(f32[4,8,4,32,128]{4,3,2,1,0:T(8,128)S(1)} %pad_maximum_fusion.1.refs_12_), channel_id=1, source_target_pairs={{0,8},{8,0},{4,12},{12,4},{16,24},{24,16},{20,28},{28,20},{32,40},... | collective-permute-start | bytes 6291464 | tf_op jit(solution)/shard_map/ppermute | solution.py:29
  154.3 24.7 %collective-permute-start.29 = (f32[2,8,4,32,128]{4,3,2,1,0:T(8,128)S(1)}, f32[2,8,4,32,128]{4,3,2,1,0:T(8,128)S(1)}, u32[]{:S(2)}, u32[]{:S(2)}) collective-permute-start(f32[2,8,4,32,128]{4,3,2,1,0:T(8,128)S(1)} %slice.55), channel_id=1, source_target_pairs={{0,192},{8,200},{4,196},{12,204},{16,208},{24,216},{20,212},{28,22... | collective-permute-start | bytes 3145736 | tf_op jit(solution)/shard_map/ppermute | solution.py:29
  156.6 31.3 %collective-permute-start.22 = (f32[2,8,5,32,128]{4,3,2,1,0:T(8,128)S(1)}, f32[2,8,5,32,128]{4,3,2,1,0:T(8,128)}, u32[]{:S(2)}, u32[]{:S(2)}) collective-permute-start(f32[2,8,5,32,128]{4,3,2,1,0:T(8,128)S(1)} %slice.53), channel_id=1, source_target_pairs={{0,3},{8,11},{4,7},{12,15},{16,19},{24,27},{20,23},{28,31},{32,35}... | collective-permute-start | bytes 3932168 | tf_op jit(solution)/shard_map/ppermute | solution.py:29
  158.2 30.5 %collective-permute-start.21 = (f32[2,8,5,32,128]{4,3,2,1,0:T(8,128)S(1)}, f32[2,8,5,32,128]{4,3,2,1,0:T(8,128)}, u32[]{:S(2)}, u32[]{:S(2)}) collective-permute-start(f32[2,8,5,32,128]{4,3,2,1,0:T(8,128)S(1)} %slice.52), channel_id=1, source_target_pairs={{0,1},{8,9},{4,5},{12,13},{16,17},{24,25},{20,21},{28,29},{32,33},... | collective-permute-start | bytes 3932168 | tf_op jit(solution)/shard_map/ppermute | solution.py:29
  162.8 25.1 %collective-permute-start.28 = (f32[2,8,4,32,128]{4,3,2,1,0:T(8,128)S(1)}, f32[2,8,4,32,128]{4,3,2,1,0:T(8,128)S(1)}, u32[]{:S(2)}, u32[]{:S(2)}) collective-permute-start(f32[2,8,4,32,128]{4,3,2,1,0:T(8,128)S(1)} %slice.54), channel_id=1, source_target_pairs={{0,64},{8,72},{4,68},{12,76},{16,80},{24,88},{20,84},{28,92},{32,9... | collective-permute-start | bytes 3145736 | tf_op jit(solution)/shard_map/ppermute | solution.py:29
  164.1 35.2 %collective-permute-start.31 = (f32[4,8,4,32,128]{4,3,2,1,0:T(8,128)}, f32[4,8,4,32,128]{4,3,2,1,0:T(8,128)}, u32[]{:S(2)}, u32[]{:S(2)}) collective-permute-start(f32[4,8,4,32,128]{4,3,2,1,0:T(8,128)} %collective-permute-done.19.refs_13_), channel_id=1, source_target_pairs={{0,8},{8,0},{4,12},{12,4},{16,24},{24,16},{20,28},{28,20},{32,40},... | collective-permute-start | bytes 6291464 | tf_op jit(solution)/shard_map/ppermute | solution.py:29
  179.0 9.7 %collective-permute-start.34 = (f32[2,8,4,32,128]{4,3,2,1,0:T(8,128)S(1)}, f32[2,8,4,32,128]{4,3,2,1,0:T(8,128)S(1)}, u32[]{:S(2)}, u32[]{:S(2)}) collective-permute-start(f32[2,8,4,32,128]{4,3,2,1,0:T(8,128)S(1)} %collective-permute-done.29.refs_16_), channel_id=1, source_target_pairs={{0,8},{8,0},{4,12},{12,4},{16,24},{24,16},{20,28},{28,20},{32,40},... | collective-permute-start | bytes 3145736 | tf_op jit(solution)/shard_map/ppermute | solution.py:29
  187.8 17.3 %collective-permute-start.24 = (f32[4,8,5,32,128]{4,3,2,1,0:T(8,128)}, f32[4,8,5,32,128]{4,3,2,1,0:T(8,128)}, u32[]{:S(2)}, u32[]{:S(2)}) collective-permute-start(f32[4,8,5,32,128]{4,3,2,1,0:T(8,128)} %collective-permute-done.17.refs_3_), channel_id=1, source_target_pairs={{0,8},{8,0},{4,12},{12,4},{16,24},{24,16},{20,28},{28,20},{32,40},... | collective-permute-start | bytes 7864328 | tf_op jit(solution)/shard_map/ppermute | solution.py:29
  188.0 17.1 %collective-permute-start.25 = (f32[4,8,5,32,128]{4,3,2,1,0:T(8,128)}, f32[4,8,5,32,128]{4,3,2,1,0:T(8,128)}, u32[]{:S(2)}, u32[]{:S(2)}) collective-permute-start(f32[4,8,5,32,128]{4,3,2,1,0:T(8,128)} %collective-permute-done.18.refs_4_), channel_id=1, source_target_pairs={{0,8},{8,0},{4,12},{12,4},{16,24},{24,16},{20,28},{28,20},{32,40},... | collective-permute-start | bytes 7864328 | tf_op jit(solution)/shard_map/ppermute | solution.py:29
  188.6 9.6 %collective-permute-start.33 = (f32[2,8,4,32,128]{4,3,2,1,0:T(8,128)S(1)}, f32[2,8,4,32,128]{4,3,2,1,0:T(8,128)S(1)}, u32[]{:S(2)}, u32[]{:S(2)}) collective-permute-start(f32[2,8,4,32,128]{4,3,2,1,0:T(8,128)S(1)} %collective-permute-done.28.refs_15_), channel_id=1, source_target_pairs={{0,8},{8,0},{4,12},{12,4},{16,24},{24,16},{20,28},{28,20},{32,40},... | collective-permute-start | bytes 3145736 | tf_op jit(solution)/shard_map/ppermute | solution.py:29
  188.7 12.7 %collective-permute-start.32 = (f32[4,8,4,32,128]{4,3,2,1,0:T(8,128)}, f32[4,8,4,32,128]{4,3,2,1,0:T(8,128)}, u32[]{:S(2)}, u32[]{:S(2)}) collective-permute-start(f32[4,8,4,32,128]{4,3,2,1,0:T(8,128)} %collective-permute-done.20.refs_14_), channel_id=1, source_target_pairs={{0,8},{8,0},{4,12},{12,4},{16,24},{24,16},{20,28},{28,20},{32,40},... | collective-permute-start | bytes 6291464 | tf_op jit(solution)/shard_map/ppermute | solution.py:29
  199.3 5.8 %collective-permute-start.26 = (f32[2,8,5,32,128]{4,3,2,1,0:T(8,128)}, f32[2,8,5,32,128]{4,3,2,1,0:T(8,128)}, u32[]{:S(2)}, u32[]{:S(2)}) collective-permute-start(f32[2,8,5,32,128]{4,3,2,1,0:T(8,128)} %collective-permute-done.21.refs_5_), channel_id=1, source_target_pairs={{0,8},{8,0},{4,12},{12,4},{16,24},{24,16},{20,28},{28,20},{32,40},... | collective-permute-start | bytes 3932168 | tf_op jit(solution)/shard_map/ppermute | solution.py:29
  (7 other events, 81.1 us)
